TPU v7x, 256 devices: a whole 4x4x8 slice. The times are simulated.
256 devices in a mesh: grp: 16 (over y_hi, x, core), sub: 16 (over y_lo, z).
Axes of the slice: x: 4, y: 4 (y_hi: 2, y_lo: 2; y = y_hi * 2 + y_lo), z: 8, core: 2. Of those that a mesh axis runs over, the one named last changes fastest.
Arguments:
- arrivals: float32 [128, 262144], P('sub', 'grp'), may hold values from -64 to 64
- sketch: float32 [256, 262144], P(None, ('grp', 'sub')), may hold values from -96 to 96
- owner: int32 [8192], P('grp'), may hold values from 0 to 511, as said below
- slot: int32 [128], replicated, may hold values from 0 to 127, each once
Outputs:
- final_sketch: float32 [256, 262144], P(None, ('grp', 'sub'))
- residual: float32 [128, 262144], P(None, ('grp', 'sub'))
Inputs may be any that keep to these rules, and one draw needn't show every extreme that they name: `owner`: each aligned block of 512 entries names each host of its group once. `slot`: each time step has its own arrival row.
All inputs are finite; a program needn't handle non-finite values.
Results may differ from a plain program's by a relative error of at most 0.00016.
Values sent between devices are 32-bit elements; how exact they have to be, the bound alone decides.
A program may use at most 64 MiB of HBM per device.

v0:
```python
import jax
import jax.numpy as jnp
from jax import lax
from jax.sharding import Mesh
from jax.sharding import PartitionSpec as P

ELL = 256
NEW = 64
TOP = 32
ROWS = 320
SUB = ("sub_0", "sub_1")
GRP_SUB = ("grp_0", "grp_1", "grp_2", "sub_0", "sub_1")
GRP = ("grp_0", "grp_1", "grp_2")
highest = lax.Precision.HIGHEST


def one_axis_at_a_time(x, axes):
    for axis in axes:
        x = lax.psum(x, axis)
    return x


def product(former, latter):
    return jnp.dot(former, latter, precision=highest, preferred_element_type=jnp.float32)


def symmetric(matrix):
    return 0.5 * (matrix + matrix.T)


def lower_inverse(triangle):
    identity = jnp.eye(triangle.shape[0], dtype=jnp.float32)
    return jax.scipy.linalg.solve_triangular(triangle, identity, lower=True)


def orthonormal(columns):
    factor = jnp.linalg.cholesky(symmetric(product(columns.T, columns)))
    return jax.scipy.linalg.solve_triangular(factor, columns.T, lower=True).T


def shrink_factors(gram_matrix):
    subspace = orthonormal(gram_matrix[:, :ELL])
    reduced = symmetric(product(subspace.T, product(gram_matrix, subspace)))
    inverse_root = lower_inverse(jnp.linalg.cholesky(reduced))
    offset = 0.5 / jnp.sum(inverse_root * inverse_root)
    keeper = jnp.eye(ELL, dtype=jnp.float32) - offset * product(inverse_root.T, inverse_root)
    shrink_factor = jnp.linalg.cholesky(symmetric(keeper)).T
    return (product(shrink_factor, subspace.T), shrink_factor, reduced)


def local(arrivals, sketch, owner, slot):
    arrived_rows, arrived_columns = arrivals.shape
    host_count = owner.shape[0]
    shaped = arrivals.reshape(arrived_rows, host_count, arrived_columns // host_count)
    placed = jnp.take(shaped, owner, axis=1).reshape(arrived_rows, arrived_columns)
    regrouped = lax.all_to_all(placed, SUB, split_axis=1, concat_axis=0, tiled=True)
    samples = jnp.take(regrouped, slot, axis=0)
    first_batch = samples[:NEW]
    second_batch = samples[NEW:]
    stacked = jnp.concatenate([sketch, first_batch], axis=0)
    gram_one = lax.psum(product(stacked, stacked.T), GRP_SUB)
    weights_one, factor_one, reduced_one = shrink_factors(gram_one)
    middle = product(weights_one, stacked)
    stacked_two = jnp.concatenate([middle, second_batch], axis=0)
    extended = jnp.concatenate([stacked_two, first_batch], axis=0)
    summed = one_axis_at_a_time(product(extended, second_batch.T), GRP_SUB)
    corner = symmetric(product(factor_one, product(reduced_one, factor_one.T)))
    side_block = summed[:ROWS]
    upper_rows = jnp.concatenate([corner, side_block[:ELL]], axis=1)
    gram_two = jnp.concatenate([upper_rows, side_block.T], axis=0)
    early_rows = jnp.concatenate([product(gram_one[ELL:], weights_one.T), summed[ROWS:]], axis=1)
    weights_two, factor_two, reduced_two = shrink_factors(gram_two)
    final_sketch = product(weights_two, stacked_two)
    spectrum = symmetric(product(factor_two, product(reduced_two, factor_two.T)))
    leading = orthonormal(spectrum[:, :TOP])
    directions = product(leading.T, final_sketch)
    small_gram = symmetric(product(leading.T, product(spectrum, leading)))
    inverse_root = lower_inverse(jnp.linalg.cholesky(small_gram))
    sample_rows = jnp.concatenate([early_rows, gram_two[ELL:]], axis=0)
    scores = product(sample_rows, product(weights_two.T, leading))
    coefficients = product(product(scores, inverse_root.T), inverse_root)
    residual = samples - product(coefficients, directions)
    return (final_sketch, residual)


def solution(mesh):
    split = Mesh(mesh.devices.reshape(2, 4, 2, 2, 8), ("grp_0", "grp_1", "grp_2", "sub_0", "sub_1"))
    placed = (P(SUB, GRP), P(None, GRP_SUB), P(GRP), P())
    return jax.shard_map(
        local,
        mesh=split,
        in_specs=placed,
        out_specs=(P(None, GRP_SUB), P(None, GRP_SUB)),
        check_vma=False,
    )
```

profile of v0, /device:TPU:2, one launch (start us, length us, event | category | flops | bytes accessed | tf_op | source)
XLA Modules:
  0.0 899.6 jit_solution(13229806428466531764)
XLA Ops:
  21.2 9.6 %all-to-all-start = ((f32[8,16,1024]{2,0,1:T(8,128)}), f32[8,16,1024]{2,0,1:T(8,128)S(1)}, u32[]{:S(2)}, u32[]{:S(2)}) async-start(f32[8,16,1024]{2,0,1:T(8,128)} %copy.55), calls=%async_computation | async-start | bytes 1048576 | tf_op jit(solution)/shard_map/all_to_all | solution.py:56
  31.1 15.4 %all-to-all-done = f32[8,16,1024]{2,0,1:T(8,128)S(1)} async-done(((f32[8,16,1024]{2,0,1:T(8,128)}), f32[8,16,1024]{2,0,1:T(8,128)S(1)}, u32[]{:S(2)}, u32[]{:S(2)}) %all-to-all-start) | async-done | bytes 524320 | tf_op jit(solution)/shard_map/all_to_all | solution.py:56
  52.0 253.9 %all-reduce.8.cloned.1.call-done = f32[320,320]{1,0:T(8,128)} async-done(((f32[320,320]{1,0:T(8,128)}), f32[320,320]{1,0:T(8,128)}) %all-reduce.8.cloned.1.call-update) | async-done | bytes 409616 | tf_op jit(solution)/shard_map/psum | solution.py:61
  308.2 11.7 %cholesky.340 = f32[128,128]{1,0:T(8,128)S(1)} custom-call(f32[128,128]{1,0:T(8,128)S(1)} %cholesky.562), custom_call_target="Cholesky" | custom-call | tf_op jit(solution)/shard_map/jit(cholesky)/cholesky | solution.py:37
  320.0 9.8 %custom-call.33 = f32[1,128,128]{1,2,0:T(8,128)S(1)} custom-call(f32[1,128,128]{2,1,0:T(8,128)S(1)} %get-tuple-element.103), custom_call_target="InvertDiagBlocksLowerTriangular" | custom-call | tf_op jit(solution)/shard_map/jit(cholesky)/cholesky | solution.py:37
  330.3 11.7 %cholesky.357 = f32[128,128]{1,0:T(8,128)S(1)} custom-call(f32[128,128]{1,0:T(8,128)S(1)} %convolution_subtract_fusion.10), custom_call_target="Cholesky" | custom-call | tf_op jit(solution)/shard_map/jit(cholesky)/cholesky | solution.py:37
  347.9 20.1 %custom-call.34 = f32[2,128,128]{1,2,0:T(8,128)S(1)} custom-call(f32[2,128,128]{2,1,0:T(8,128)S(1)} %get-tuple-element.34), custom_call_target="InvertDiagBlocksLowerTriangular" | custom-call | tf_op jit(solution)/shard_map/jit(_solve_triangular)/triangular_solve | solution.py:38
  370.9 11.7 %cholesky.374 = f32[128,128]{1,0:T(8,128)S(1)} custom-call(f32[128,128]{1,0:T(8,128)S(1)} %cholesky.565), custom_call_target="Cholesky" | custom-call | tf_op jit(solution)/shard_map/jit(cholesky)/cholesky | solution.py:44
  382.6 9.8 %custom-call.35 = f32[1,128,128]{1,2,0:T(8,128)S(1)} custom-call(f32[1,128,128]{2,1,0:T(8,128)S(1)} %get-tuple-element.99), custom_call_target="InvertDiagBlocksLowerTriangular" | custom-call | tf_op jit(solution)/shard_map/jit(cholesky)/cholesky | solution.py:44
  392.9 11.9 %cholesky.391 = f32[128,128]{1,0:T(8,128)S(1)} custom-call(f32[128,128]{1,0:T(8,128)S(1)} %convolution_subtract_fusion.9), custom_call_target="Cholesky" | custom-call | tf_op jit(solution)/shard_map/jit(cholesky)/cholesky | solution.py:44
  407.6 4.1 while.9
  411.7 19.7 %custom-call.36 = f32[2,128,128]{1,2,0:T(8,128)S(1)} custom-call(f32[2,128,128]{2,1,0:T(8,128)S(1)} %get-tuple-element.35), custom_call_target="InvertDiagBlocksLowerTriangular" | custom-call | tf_op jit(solution)/shard_map/jit(_solve_triangular)/triangular_solve | solution.py:33
  434.7 11.7 %cholesky.408 = f32[128,128]{1,0:T(8,128)S(1)} custom-call(f32[128,128]{1,0:T(8,128)S(1)} %cholesky.568), custom_call_target="Cholesky" | custom-call | tf_op jit(solution)/shard_map/jit(cholesky)/cholesky | solution.py:47
  446.4 9.8 %custom-call.37 = f32[1,128,128]{1,2,0:T(8,128)S(1)} custom-call(f32[1,128,128]{2,1,0:T(8,128)S(1)} %get-tuple-element.95), custom_call_target="InvertDiagBlocksLowerTriangular" | custom-call | tf_op jit(solution)/shard_map/jit(cholesky)/cholesky | solution.py:47
  456.7 11.7 %cholesky.425 = f32[128,128]{1,0:T(8,128)S(1)} custom-call(f32[128,128]{1,0:T(8,128)S(1)} %convolution_subtract_fusion.8), custom_call_target="Cholesky" | custom-call | tf_op jit(solution)/shard_map/jit(cholesky)/cholesky | solution.py:47
  477.3 31.7 %all-reduce.10.cloned.1.call-done = f32[384,64]{0,1:T(8,128)} async-done(((f32[384,64]{0,1:T(8,128)}), f32[384,64]{0,1:T(8,128)}) %all-reduce.10.cloned.1.call-update) | async-done | bytes 98320 | tf_op jit(solution)/shard_map/psum | solution.py:19
  509.7 46.3 %all-reduce.12.cloned.1.call-done = f32[384,64]{0,1:T(8,128)} async-done(((f32[384,64]{0,1:T(8,128)}), f32[384,64]{0,1:T(8,128)}) %all-reduce.12.cloned.1.call-update) | async-done | bytes 98320 | tf_op jit(solution)/shard_map/psum | solution.py:19
  556.8 32.0 %all-reduce.14.cloned.1.call-done = f32[384,64]{0,1:T(8,128)} async-done(((f32[384,64]{0,1:T(8,128)}), f32[384,64]{0,1:T(8,128)}) %all-reduce.14.cloned.1.call-update) | async-done | bytes 98320 | tf_op jit(solution)/shard_map/psum | solution.py:19
  588.9 36.5 %all-reduce.16.cloned.1.call-done = f32[384,64]{0,1:T(8,128)} async-done(((f32[384,64]{0,1:T(8,128)}), f32[384,64]{0,1:T(8,128)}) %all-reduce.16.cloned.1.call-update) | async-done | bytes 98320 | tf_op jit(solution)/shard_map/psum | solution.py:19
  627.8 73.3 %all-reduce.18.cloned.1.call-done = f32[384,64]{0,1:T(8,128)} async-done(((f32[384,64]{0,1:T(8,128)}), f32[384,64]{0,1:T(8,128)}) %all-reduce.18.cloned.1.call-update) | async-done | bytes 98320 | tf_op jit(solution)/shard_map/psum | solution.py:19
  703.9 11.7 %cholesky.442 = f32[128,128]{1,0:T(8,128)S(1)} custom-call(f32[128,128]{1,0:T(8,128)S(1)} %cholesky.571), custom_call_target="Cholesky" | custom-call | tf_op jit(solution)/shard_map/jit(cholesky)/cholesky | solution.py:37
  715.7 9.8 %custom-call.38 = f32[1,128,128]{1,2,0:T(8,128)S(1)} custom-call(f32[1,128,128]{2,1,0:T(8,128)S(1)} %get-tuple-element.91), custom_call_target="InvertDiagBlocksLowerTriangular" | custom-call | tf_op jit(solution)/shard_map/jit(cholesky)/cholesky | solution.py:37
  726.0 11.7 %cholesky.459 = f32[128,128]{1,0:T(8,128)S(1)} custom-call(f32[128,128]{1,0:T(8,128)S(1)} %convolution_subtract_fusion.7), custom_call_target="Cholesky" | custom-call | tf_op jit(solution)/shard_map/jit(cholesky)/cholesky | solution.py:37
  740.5 4.1 while.10
  744.6 19.8 %custom-call.39 = f32[2,128,128]{1,2,0:T(8,128)S(1)} custom-call(f32[2,128,128]{2,1,0:T(8,128)S(1)} %get-tuple-element.36), custom_call_target="InvertDiagBlocksLowerTriangular" | custom-call | tf_op jit(solution)/shard_map/jit(_solve_triangular)/triangular_solve | solution.py:38
  768.1 11.7 %cholesky.476 = f32[128,128]{1,0:T(8,128)S(1)} custom-call(f32[128,128]{1,0:T(8,128)S(1)} %cholesky.574), custom_call_target="Cholesky" | custom-call | tf_op jit(solution)/shard_map/jit(cholesky)/cholesky | solution.py:44
  779.8 9.8 %custom-call.40 = f32[1,128,128]{1,2,0:T(8,128)S(1)} custom-call(f32[1,128,128]{2,1,0:T(8,128)S(1)} %get-tuple-element.87), custom_call_target="InvertDiagBlocksLowerTriangular" | custom-call | tf_op jit(solution)/shard_map/jit(cholesky)/cholesky | solution.py:44
  790.1 11.9 %cholesky.493 = f32[128,128]{1,0:T(8,128)S(1)} custom-call(f32[128,128]{1,0:T(8,128)S(1)} %convolution_subtract_fusion.6), custom_call_target="Cholesky" | custom-call | tf_op jit(solution)/shard_map/jit(cholesky)/cholesky | solution.py:44
  808.7 19.7 %custom-call.41 = f32[2,128,128]{1,2,0:T(8,128)S(1)} custom-call(f32[2,128,128]{2,1,0:T(8,128)S(1)} %get-tuple-element.37), custom_call_target="InvertDiagBlocksLowerTriangular" | custom-call | tf_op jit(solution)/shard_map/jit(_solve_triangular)/triangular_solve | solution.py:33
  831.9 11.7 %cholesky.510 = f32[128,128]{1,0:T(8,128)S(1)} custom-call(f32[128,128]{1,0:T(8,128)S(1)} %cholesky.577), custom_call_target="Cholesky" | custom-call | tf_op jit(solution)/shard_map/jit(cholesky)/cholesky | solution.py:47
  843.7 9.8 %custom-call.42 = f32[1,128,128]{1,2,0:T(8,128)S(1)} custom-call(f32[1,128,128]{2,1,0:T(8,128)S(1)} %get-tuple-element.83), custom_call_target="InvertDiagBlocksLowerTriangular" | custom-call | tf_op jit(solution)/shard_map/jit(cholesky)/cholesky | solution.py:47
  854.0 11.7 %cholesky.527 = f32[128,128]{1,0:T(8,128)S(1)} custom-call(f32[128,128]{1,0:T(8,128)S(1)} %convolution_subtract_fusion.5), custom_call_target="Cholesky" | custom-call | tf_op jit(solution)/shard_map/jit(cholesky)/cholesky | solution.py:47
  (234 shorter events, 104.6 us)
Async XLA Ops:
  20.1 10.9 %copy-start.9 = (s32[128]{0:T(128)S(1)}, s32[128]{0:T(128)}, u32[]{:S(2)}) copy-start(s32[128]{0:T(128)} %param.13) | copy-start | bytes 1540
  21.2 25.3 %all-to-all-start = ((f32[8,16,1024]{2,0,1:T(8,128)}), f32[8,16,1024]{2,0,1:T(8,128)S(1)}, u32[]{:S(2)}, u32[]{:S(2)}) async-start(f32[8,16,1024]{2,0,1:T(8,128)} %copy.55), calls=%async_computation | async-start | bytes 1048576 | tf_op jit(solution)/shard_map/all_to_all | solution.py:56
  30.8 275.0 %all-reduce.8.cloned.1.call-start = ((), (), s32[]{:S(2)}) async-start(), calls=%async_computation.1 | async-start | bytes 983040 | tf_op jit(solution)/shard_map/psum | solution.py:61
  47.3 1.3 copy-start
  48.2 259.7 %copy-start.5 = (f32[64,1024]{1,0:T(8,128)}, f32[64,1024]{1,0:T(8,128)S(1)}, u32[]{:S(2)}) copy-start(f32[64,1024]{1,0:T(8,128)S(1)} %get-tuple-element.78) | copy-start | bytes 786436
  51.7 457.4 %all-reduce.10.cloned.1.call-start = ((), (), s32[]{:S(2)}) async-start(), calls=%async_computation.2 | async-start | bytes 196608 | tf_op jit(solution)/shard_map/psum | solution.py:19
  52.0 379.7 %copy-start.3 = (f32[256,256]{1,0:T(8,128)}, f32[256,256]{1,0:T(8,128)S(1)}, u32[]{:S(2)}) copy-start(f32[256,256]{1,0:T(8,128)S(1)} %fusion.36) | copy-start | bytes 786436
  308.2 59.8 %copy-start.2 = (f32[320,320]{1,0:T(8,128)S(1)}, f32[320,320]{1,0:T(8,128)}, u32[]{:S(2)}) copy-start(f32[320,320]{1,0:T(8,128)} %all-reduce.8.cloned.1.call-done) | copy-start | bytes 1228804
  472.1 2.9 copy-start.6
  472.1 2.9 copy-start.7
  477.2 78.8 %all-reduce.12.cloned.1.call-start = ((), (), s32[]{:S(2)}) async-start(), calls=%async_computation.3 | async-start | bytes 196608 | tf_op jit(solution)/shard_map/psum | solution.py:19
  509.1 79.7 %all-reduce.14.cloned.1.call-start = ((), (), s32[]{:S(2)}) async-start(), calls=%async_computation.4 | async-start | bytes 196608 | tf_op jit(solution)/shard_map/psum | solution.py:19
  556.1 69.3 %all-reduce.16.cloned.1.call-start = ((), (), s32[]{:S(2)}) async-start(), calls=%async_computation.5 | async-start | bytes 196608 | tf_op jit(solution)/shard_map/psum | solution.py:19
  588.8 112.2 %all-reduce.18.cloned.1.call-start = ((), (), s32[]{:S(2)}) async-start(), calls=%async_computation.6 | async-start | bytes 196608 | tf_op jit(solution)/shard_map/psum | solution.py:19
  768.0 60.4 %copy-start.4 = (f32[256,256]{1,0:T(8,128)S(1)}, f32[256,256]{1,0:T(8,128)}, u32[]{:S(2)}) copy-start(f32[256,256]{1,0:T(8,128)} %copy-done.3) | copy-start | bytes 786436
  880.6 11.7 %copy-start.1 = (f32[256,1024]{1,0:T(8,128)}, f32[256,1024]{1,0:T(8,128)S(1)}, u32[]{:S(2)}) copy-start(f32[256,1024]{1,0:T(8,128)S(1)} %fusion.6) | copy-start | bytes 3145732
  880.6 9.6 %copy-start.8 = (f32[64,256]{0,1:T(8,128)S(1)}, f32[64,256]{0,1:T(8,128)}, u32[]{:S(2)}) copy-start(f32[64,256]{0,1:T(8,128)} %fusion.85) | copy-start | bytes 196612
Sparse Core Ops, SparseCore 0:
  51.8 254.0 all-reduce.7
  477.4 31.6 all-reduce.9
  511.4 44.6 all-reduce.11
  558.5 30.2 all-reduce.13
  591.1 34.1 all-reduce.15
  627.6 73.4 all-reduce.17
where the time goes:
time: 906 us; the launch traced here: 900 us
  waiting for transfers between devices  489 us (54%)
  other arithmetic  304 us (34%)
  local copies, waits for them, and re-layouts  35.8 us (4%)
  matrix products  35.2 us (4%)
  between operations  24.8 us (3%)
  starting transfers between devices  10 us (1%)
    psum x1, waiting for transfers between devices, local(): gram_one = lax.psum(product(stacked, stacked.T), GRP_SUB)  254 us
    psum x5, waiting for transfers between devices, one_axis_at_a_time(): x = lax.psum(x, axis)  220 us
    another operation x16, other arithmetic, orthonormal(): factor = jnp.linalg.cholesky(symmetric(product(columns.T, columns)))  72.3 us
    another operation x14, other arithmetic, shrink_factors(): inverse_root = lower_inverse(jnp.linalg.cholesky(reduced))  69.7 us
    another operation x14, other arithmetic, shrink_factors(): shrink_factor = jnp.linalg.cholesky(symmetric(keeper)).T  69.3 us
    another operation x7, other arithmetic, orthonormal(): return jax.scipy.linalg.solve_triangular(factor, columns.T, lower=True).T  43.2 us
    another operation x6, other arithmetic, lower_inverse(): return jax.scipy.linalg.solve_triangular(triangle, identity, lower=True)  42.5 us
    dot_general x28, matrix products, product(): jnp.dot(former, latter, precision=highest, preferred_element_type=jnp.flo...  28 us
  transfers between devices with their start and end apart: 7, of which 7 were waited for; matrix products, arithmetic and copies ran while one was open for 0% of the time, Pallas kernels for 0%

commit v1 on v0

--- a/solution.py
+++ b/solution.py
@@ -16,7 +16,8 @@
 
 def one_axis_at_a_time(x, axes):
     for axis in axes:
-        x = lax.psum(x, axis)
+        terms = lax.all_gather(x, axis)
+        x = jnp.sum(terms, axis=0)
     return x
 
 

time: 906 us -> 767 us (0.85)
  waiting for transfers between devices: 489 us -> 269 us
  blocking collectives: 0 us -> 53.6 us
  matrix products: 35.2 us -> 48.3 us
  other arithmetic: 304 us -> 314 us
    psum x5 -> x0, waiting for transfers between devices: 220 us -> none  [one_axis_at_a_time(): x = lax.psum(x, axis)]
    all_gather x0 -> x5, blocking collectives: none -> 53.6 us  [one_axis_at_a_time(): terms = lax.all_gather(x, axis)]
  transfers between devices with their start and end apart: 7 -> 2, of which waited for: 7 -> 2; matrix products, arithmetic and copies ran while one was open for 0% -> 0% of each run, Pallas kernels for 0% -> 0%
where the time goes in v1:
time: 767 us; the launch traced here: 761 us
  other arithmetic  314 us (41%)
  waiting for transfers between devices  269 us (35%)
  blocking collectives  53.6 us (7%)
  matrix products  48.3 us (6%)
  local copies, waits for them, and re-layouts  42.2 us (6%)
  between operations  24.6 us (3%)
  starting transfers between devices  9.84 us (1%)
    psum x1, waiting for transfers between devices, local(): gram_one = lax.psum(product(stacked, stacked.T), GRP_SUB)  254 us
    another operation x16, other arithmetic, orthonormal(): factor = jnp.linalg.cholesky(symmetric(product(columns.T, columns)))  72.8 us
    another operation x14, other arithmetic, shrink_factors(): inverse_root = lower_inverse(jnp.linalg.cholesky(reduced))  69.6 us
    another operation x14, other arithmetic, shrink_factors(): shrink_factor = jnp.linalg.cholesky(symmetric(keeper)).T  69.2 us
    all_gather x5, blocking collectives, one_axis_at_a_time(): terms = lax.all_gather(x, axis)  53.6 us
    another operation x6, other arithmetic, lower_inverse(): return jax.scipy.linalg.solve_triangular(triangle, identity, lower=True)  45 us
    another operation x7, other arithmetic, orthonormal(): return jax.scipy.linalg.solve_triangular(factor, columns.T, lower=True).T  44.3 us
    dot_general x28, matrix products, product(): jnp.dot(former, latter, precision=highest, preferred_element_type=jnp.flo...  29.4 us
  transfers between devices with their start and end apart: 2, of which 2 were waited for; matrix products, arithmetic and copies ran while one was open for 0% of the time, Pallas kernels for 0%

profile of v1, /device:TPU:2, one launch (start us, length us, event | category | flops | bytes accessed | tf_op | source)
XLA Modules:
  0.0 761.1 jit_solution(12705334473970715213)
XLA Ops:
  21.2 9.6 %all-to-all-start = ((f32[8,16,1024]{2,0,1:T(8,128)}), f32[8,16,1024]{2,0,1:T(8,128)S(1)}, u32[]{:S(2)}, u32[]{:S(2)}) async-start(f32[8,16,1024]{2,0,1:T(8,128)} %copy.136), calls=%async_computation | async-start | bytes 1048576 | tf_op jit(solution)/shard_map/all_to_all | solution.py:57
  32.0 14.5 %all-to-all-done = f32[8,16,1024]{2,0,1:T(8,128)S(1)} async-done(((f32[8,16,1024]{2,0,1:T(8,128)}), f32[8,16,1024]{2,0,1:T(8,128)S(1)}, u32[]{:S(2)}, u32[]{:S(2)}) %all-to-all-start) | async-done | bytes 524320 | tf_op jit(solution)/shard_map/all_to_all | solution.py:57
  51.7 254.1 %all-reduce.3.cloned.1.call-done = f32[320,320]{1,0:T(8,128)} async-done(((f32[320,320]{1,0:T(8,128)}), f32[320,320]{1,0:T(8,128)}) %all-reduce.3.cloned.1.call-update) | async-done | bytes 409616 | tf_op jit(solution)/shard_map/psum | solution.py:62
  308.2 11.7 %cholesky.340 = f32[128,128]{1,0:T(8,128)S(1)} custom-call(f32[128,128]{1,0:T(8,128)S(1)} %cholesky.562), custom_call_target="Cholesky" | custom-call | tf_op jit(solution)/shard_map/jit(cholesky)/cholesky | solution.py:38
  320.0 9.8 %custom-call.33 = f32[1,128,128]{1,2,0:T(8,128)S(1)} custom-call(f32[1,128,128]{2,1,0:T(8,128)S(1)} %get-tuple-element.103), custom_call_target="InvertDiagBlocksLowerTriangular" | custom-call | tf_op jit(solution)/shard_map/jit(cholesky)/cholesky | solution.py:38
  330.3 12.2 %cholesky.357 = f32[128,128]{1,0:T(8,128)S(1)} custom-call(f32[128,128]{1,0:T(8,128)S(1)} %convolution_subtract_fusion.10), custom_call_target="Cholesky" | custom-call | tf_op jit(solution)/shard_map/jit(cholesky)/cholesky | solution.py:38
  348.7 19.7 %custom-call.34 = f32[2,128,128]{1,2,0:T(8,128)S(1)} custom-call(f32[2,128,128]{2,1,0:T(8,128)S(1)} %get-tuple-element.34), custom_call_target="InvertDiagBlocksLowerTriangular" | custom-call | tf_op jit(solution)/shard_map/jit(_solve_triangular)/triangular_solve | solution.py:39
  373.6 11.7 %cholesky.374 = f32[128,128]{1,0:T(8,128)S(1)} custom-call(f32[128,128]{1,0:T(8,128)S(1)} %cholesky.565), custom_call_target="Cholesky" | custom-call | tf_op jit(solution)/shard_map/jit(cholesky)/cholesky | solution.py:45
  385.4 9.8 %custom-call.35 = f32[1,128,128]{1,2,0:T(8,128)S(1)} custom-call(f32[1,128,128]{2,1,0:T(8,128)S(1)} %get-tuple-element.99), custom_call_target="InvertDiagBlocksLowerTriangular" | custom-call | tf_op jit(solution)/shard_map/jit(cholesky)/cholesky | solution.py:45
  397.4 11.9 %cholesky.391 = f32[128,128]{1,0:T(8,128)S(1)} custom-call(f32[128,128]{1,0:T(8,128)S(1)} %convolution_subtract_fusion.9), custom_call_target="Cholesky" | custom-call | tf_op jit(solution)/shard_map/jit(cholesky)/cholesky | solution.py:45
  412.9 4.1 while.9
  417.0 19.7 %custom-call.36 = f32[2,128,128]{1,2,0:T(8,128)S(1)} custom-call(f32[2,128,128]{2,1,0:T(8,128)S(1)} %get-tuple-element.35), custom_call_target="InvertDiagBlocksLowerTriangular" | custom-call | tf_op jit(solution)/shard_map/jit(_solve_triangular)/triangular_solve | solution.py:34
  443.1 11.7 %cholesky.408 = f32[128,128]{1,0:T(8,128)S(1)} custom-call(f32[128,128]{1,0:T(8,128)S(1)} %cholesky.568), custom_call_target="Cholesky" | custom-call | tf_op jit(solution)/shard_map/jit(cholesky)/cholesky | solution.py:48
  454.9 9.8 %custom-call.37 = f32[1,128,128]{1,2,0:T(8,128)S(1)} custom-call(f32[1,128,128]{2,1,0:T(8,128)S(1)} %get-tuple-element.95), custom_call_target="InvertDiagBlocksLowerTriangular" | custom-call | tf_op jit(solution)/shard_map/jit(cholesky)/cholesky | solution.py:48
  466.9 11.7 %cholesky.425 = f32[128,128]{1,0:T(8,128)S(1)} custom-call(f32[128,128]{1,0:T(8,128)S(1)} %convolution_subtract_fusion.8), custom_call_target="Cholesky" | custom-call | tf_op jit(solution)/shard_map/jit(cholesky)/cholesky | solution.py:48
  488.6 6.8 all-gather
  495.7 13.0 %all-gather.1 = f32[1536,64]{0,1:T(8,128)S(1)} all-gather(f32[384,64]{0,1:T(8,128)S(1)} %reduce_sum.64), channel_id=3, replica_groups=mesh['grp_0'=2,'grp_1'=4,'grp_2'=2,'sub_0'=2,'sub_1'=8] {'grp_1'}, dimensions={0}, use_global_device_ids=true | all-gather | bytes 491520 | tf_op jit(solution)/shard_map/all_gather | solution.py:19
  511.4 5.5 all-gather.3
  517.3 26.3 %all-gather.4 = f32[3072,64]{0,1:T(8,128)S(1)} all-gather(f32[384,64]{0,1:T(8,128)S(1)} %reduce_sum.67), channel_id=6, replica_groups=mesh['grp_0'=2,'grp_1'=4,'grp_2'=2,'sub_0'=2,'sub_1'=8] {'sub_1'}, dimensions={0}, use_global_device_ids=true | all-gather | bytes 884736 | tf_op jit(solution)/shard_map/all_gather | solution.py:19
  546.5 11.7 %cholesky.442 = f32[128,128]{1,0:T(8,128)S(1)} custom-call(f32[128,128]{1,0:T(8,128)S(1)} %cholesky.571), custom_call_target="Cholesky" | custom-call | tf_op jit(solution)/shard_map/jit(cholesky)/cholesky | solution.py:38
  558.3 9.8 %custom-call.38 = f32[1,128,128]{1,2,0:T(8,128)S(1)} custom-call(f32[1,128,128]{2,1,0:T(8,128)S(1)} %get-tuple-element.91), custom_call_target="InvertDiagBlocksLowerTriangular" | custom-call | tf_op jit(solution)/shard_map/jit(cholesky)/cholesky | solution.py:38
  570.3 11.7 %cholesky.459 = f32[128,128]{1,0:T(8,128)S(1)} custom-call(f32[128,128]{1,0:T(8,128)S(1)} %convolution_subtract_fusion.7), custom_call_target="Cholesky" | custom-call | tf_op jit(solution)/shard_map/jit(cholesky)/cholesky | solution.py:38
  585.7 4.1 while.10
  589.7 20.4 %custom-call.39 = f32[2,128,128]{1,2,0:T(8,128)} custom-call(f32[2,128,128]{2,1,0:T(8,128)S(1)} %get-tuple-element.36), custom_call_target="InvertDiagBlocksLowerTriangular" | custom-call | tf_op jit(solution)/shard_map/jit(_solve_triangular)/triangular_solve | solution.py:39
  616.2 11.7 %cholesky.476 = f32[128,128]{1,0:T(8,128)S(1)} custom-call(f32[128,128]{1,0:T(8,128)S(1)} %cholesky.574), custom_call_target="Cholesky" | custom-call | tf_op jit(solution)/shard_map/jit(cholesky)/cholesky | solution.py:45
  628.0 9.8 %custom-call.40 = f32[1,128,128]{1,2,0:T(8,128)S(1)} custom-call(f32[1,128,128]{2,1,0:T(8,128)S(1)} %get-tuple-element.87), custom_call_target="InvertDiagBlocksLowerTriangular" | custom-call | tf_op jit(solution)/shard_map/jit(cholesky)/cholesky | solution.py:45
  639.9 11.9 %cholesky.493 = f32[128,128]{1,0:T(8,128)S(1)} custom-call(f32[128,128]{1,0:T(8,128)S(1)} %convolution_subtract_fusion.6), custom_call_target="Cholesky" | custom-call | tf_op jit(solution)/shard_map/jit(cholesky)/cholesky | solution.py:45
  655.5 4.1 while.11
  659.6 20.3 %custom-call.41 = f32[2,128,128]{1,2,0:T(8,128)} custom-call(f32[2,128,128]{2,1,0:T(8,128)S(1)} %get-tuple-element.37), custom_call_target="InvertDiagBlocksLowerTriangular" | custom-call | tf_op jit(solution)/shard_map/jit(_solve_triangular)/triangular_solve | solution.py:34
  689.0 11.7 %cholesky.510 = f32[128,128]{1,0:T(8,128)S(1)} custom-call(f32[128,128]{1,0:T(8,128)S(1)} %cholesky.577), custom_call_target="Cholesky" | custom-call | tf_op jit(solution)/shard_map/jit(cholesky)/cholesky | solution.py:48
  700.8 9.8 %custom-call.42 = f32[1,128,128]{1,2,0:T(8,128)S(1)} custom-call(f32[1,128,128]{2,1,0:T(8,128)S(1)} %get-tuple-element.83), custom_call_target="InvertDiagBlocksLowerTriangular" | custom-call | tf_op jit(solution)/shard_map/jit(cholesky)/cholesky | solution.py:48
  712.8 11.7 %cholesky.527 = f32[128,128]{1,0:T(8,128)S(1)} custom-call(f32[128,128]{1,0:T(8,128)S(1)} %convolution_subtract_fusion.5), custom_call_target="Cholesky" | custom-call | tf_op jit(solution)/shard_map/jit(cholesky)/cholesky | solution.py:48
  (254 shorter events, 130.2 us)
Async XLA Ops:
  20.1 11.8 %copy-start.19 = (s32[128]{0:T(128)S(1)}, s32[128]{0:T(128)}, u32[]{:S(2)}) copy-start(s32[128]{0:T(128)} %param.13) | copy-start | bytes 1540
  21.2 25.3 %all-to-all-start = ((f32[8,16,1024]{2,0,1:T(8,128)}), f32[8,16,1024]{2,0,1:T(8,128)S(1)}, u32[]{:S(2)}, u32[]{:S(2)}) async-start(f32[8,16,1024]{2,0,1:T(8,128)} %copy.136), calls=%async_computation | async-start | bytes 1048576 | tf_op jit(solution)/shard_map/all_to_all | solution.py:57
  30.8 275.0 %all-reduce.3.cloned.1.call-start = ((), (), s32[]{:S(2)}) async-start(), calls=%async_computation.1 | async-start | bytes 983040 | tf_op jit(solution)/shard_map/psum | solution.py:62
  47.3 1.3 copy-start
  48.2 259.7 %copy-start.6 = (f32[64,1024]{1,0:T(8,128)}, f32[64,1024]{1,0:T(8,128)S(1)}, u32[]{:S(2)}) copy-start(f32[64,1024]{1,0:T(8,128)S(1)} %get-tuple-element.78) | copy-start | bytes 786436
  51.7 385.3 %copy-start.4 = (f32[256,256]{1,0:T(8,128)}, f32[256,256]{1,0:T(8,128)S(1)}, u32[]{:S(2)}) copy-start(f32[256,256]{1,0:T(8,128)S(1)} %fusion.36) | copy-start | bytes 786436
  308.2 60.2 %copy-start.2 = (f32[320,320]{1,0:T(8,128)S(1)}, f32[320,320]{1,0:T(8,128)}, u32[]{:S(2)}) copy-start(f32[320,320]{1,0:T(8,128)} %all-reduce.3.cloned.1.call-done) | copy-start | bytes 1228804
  372.9 0.7 copy-start.17
  409.3 2.6 copy-start.9
  442.4 0.7 copy-start.15
  483.9 3.0 copy-start.7
  483.9 3.0 copy-start.12
  543.9 1.5 copy-start.13
  545.8 0.7 copy-start.16
  546.5 63.6 %copy-start.8 = (f32[256,320]{1,0:T(8,128)S(1)}, f32[256,320]{1,0:T(8,128)}, u32[]{:S(2)}) copy-start(f32[256,320]{1,0:T(8,128)} %fusion.39) | copy-start | bytes 983044
  582.0 2.6 copy-start.10
  615.5 0.7 copy-start.18
  616.2 63.7 %copy-start.5 = (f32[256,256]{1,0:T(8,128)S(1)}, f32[256,256]{1,0:T(8,128)}, u32[]{:S(2)}) copy-start(f32[256,256]{1,0:T(8,128)} %copy-done.4) | copy-start | bytes 786436
  651.9 2.6 copy-start.11
  688.3 0.7 copy-start.14
  740.2 11.8 %copy-start.1 = (f32[256,1024]{1,0:T(8,128)}, f32[256,1024]{1,0:T(8,128)S(1)}, u32[]{:S(2)}) copy-start(f32[256,1024]{1,0:T(8,128)S(1)} %fusion.6) | copy-start | bytes 3145732
  740.2 10.7 %copy-start.3 = (f32[256,320]{0,1:T(8,128)S(1)}, f32[256,320]{0,1:T(8,128)}, u32[]{:S(2)}) copy-start(f32[256,320]{0,1:T(8,128)} %fusion.43) | copy-start | bytes 983044
Sparse Core Ops, SparseCore 0:
  51.8 254.0 all-reduce.2
